TPU v7x, 32 devices: a whole 2x2x4 slice. The times are simulated.
32 devices in a mesh: rows: 8 (over z, y), groups: 4 (over x, core).
Axes of the slice: x: 2, y: 2, z: 4, core: 2. Of those that a mesh axis runs over, the one named last changes fastest.
Arguments:
- basis: bfloat16 [8, 131072, 128], P(None, ('rows', 'groups')), may hold values from -6 to 6
- image: bfloat16 [8, 131072, 128], P(None, ('rows', 'groups')), may hold values from -6 to 6
- selection: int32 [8, 64], replicated, may hold values from 0 to 127, all different within a row
Outputs:
- rotated: bfloat16 [8, 131072, 128], P(None, ('rows', 'groups'))
Inputs may be any that keep to these rules, and one draw needn't show every extreme that they name: Each row of selection names 64 different columns.
All inputs are finite; a program needn't handle non-finite values.
Results may differ from a plain program's by a relative error of at most 0.005.
Values may be sent and summed in bfloat16 or wider, within the bound.
A program may use at most 128 MiB of HBM per device.

v0:
```python
import functools

import jax
import jax.numpy as jnp
from jax import lax
from jax.experimental import pallas as pl
from jax.experimental.pallas import tpu as pltpu
from jax.sharding import PartitionSpec as P

ITERS = 3
PANEL = 8
MESH = pl.DeviceIdType.MESH
NT = (((1,), (1,)), ((), ()))
TN = (((0,), (0,)), ((), ()))
HIGHEST = lax.Precision.HIGHEST


def exact_dot(a, b, dims=(((1,), (0,)), ((), ()))):
    return lax.dot_general(a, b, dims, precision=HIGHEST, preferred_element_type=jnp.float32)


def panel_rows(rows, first, forward):
    lanes = rows.shape[1]
    place = lax.broadcasted_iota(jnp.int32, (PANEL, 128), 0)
    wide = lax.broadcasted_iota(jnp.int32, (PANEL, lanes), 0)
    cols = [
        jnp.broadcast_to(rows[:, first + k : first + k + 1], (PANEL, 128)) for k in range(PANEL)
    ]
    full = rows
    lower = rows
    scales = []
    for j in range(PANEL):
        pivot = jnp.broadcast_to(cols[j][j : j + 1, :], (PANEL, 128))
        inv = 1.0 / pivot
        inv_wide = jnp.concatenate([inv] * (lanes // 128), axis=1)
        col_wide = jnp.concatenate([cols[j]] * (lanes // 128), axis=1)
        unit = jnp.broadcast_to(full[j : j + 1, :], full.shape) * inv_wide
        if forward:
            step = jnp.broadcast_to(lower[j : j + 1, :], lower.shape) * inv_wide
            lower = jnp.where(wide > j, lower - col_wide * step, lower)
            scales.append(pivot)
        full = jnp.where(wide == j, unit, full - col_wide * unit)
        for k in range(j + 1, PANEL):
            part = jnp.broadcast_to(cols[k][j : j + 1, :], (PANEL, 128)) * inv
            cols[k] = jnp.where(place == j, part, cols[k] - cols[j] * part)
    if not forward:
        return full, None
    pivots = scales[0]
    for j in range(1, PANEL):
        pivots = jnp.where(place == j, scales[j], pivots)
    root = lax.rsqrt(pivots)
    return full, lower * jnp.concatenate([root] * (lanes // 128), axis=1)


def solve_spd(work):
    n, lanes = work.shape
    for p in range(n // PANEL):
        first = p * PANEL
        full, _ = panel_rows(work[first : first + PANEL], first, False)
        moved = work
        for k in range(PANEL):
            moved = moved - work[:, first + k : first + k + 1] * full[k : k + 1, :]
        pieces = [moved[:first], full, moved[first + PANEL :]]
        work = jnp.concatenate([x for x in pieces if x.shape[0]], axis=0)
    return work[:, 128:]


def whiten(work):
    n, lanes = work.shape
    out = []
    for p in range(n // PANEL):
        first = p * PANEL
        full, lower = panel_rows(work[:PANEL], first, True)
        out.append(lower[:, 128:])
        work = work[PANEL:]
        if work.shape[0]:
            moved = work
            for k in range(PANEL):
                moved = moved - work[:, first + k : first + k + 1] * full[k : k + 1, :]
            work = moved
    return jnp.concatenate(out, axis=0)


def small_solve(gram_s, cross, gram_f, start, total_rows):
    width = gram_s.shape[0]
    keep = start.shape[0]
    across = solve_spd(jnp.concatenate([gram_f, cross.T], axis=1))
    turned = across.T
    coeffs = start
    for step in range(ITERS):
        solved = exact_dot(coeffs, turned)
        metric = exact_dot(exact_dot(solved, gram_s), solved, NT) / total_rows
        pad = jnp.zeros((keep, 128 - keep), jnp.float32)
        coeffs = whiten(jnp.concatenate([metric, pad, solved], axis=1))
    return coeffs


def pack(gram, width):
    gram_s = gram[:width, :width]
    gram_f = gram[width:, width:]
    row = lax.broadcasted_iota(jnp.int32, (width, width), 0)
    col = lax.broadcasted_iota(jnp.int32, (width, width), 1)
    mixed = jnp.where(row < col, gram_s, gram_f)
    diag = jnp.sum(jnp.where(row == col, gram_s, 0.0), axis=0, keepdims=True)
    return gram[:width, width:], mixed, jnp.broadcast_to(diag, (8, width))


def unpack(packed, width):
    cross = packed[:width]
    mixed = packed[width : 2 * width]
    diag = packed[2 * width : 2 * width + 1]
    row = lax.broadcasted_iota(jnp.int32, (width, width), 0)
    col = lax.broadcasted_iota(jnp.int32, (width, width), 1)
    turned = mixed.T
    gram_s = jnp.where(row < col, mixed, jnp.where(row > col, turned, diag))
    gram_f = jnp.where(row < col, turned, mixed)
    return gram_s, cross, gram_f


def place_of(nsys, n_rows, n_groups):
    inner = nsys // n_groups
    me_r = lax.axis_index("rows")
    me_g = lax.axis_index("groups")
    return me_r // inner, lax.rem(me_r, inner), me_g // 2, lax.rem(me_g, 2)


def system_at(nsys, n_rows, n_groups, step):
    half, inner, n_x = nsys // 2, nsys // n_groups, n_groups // 2
    z, y, x, c = place_of(nsys, n_rows, n_groups)
    rest = lax.rem(step, half)
    core = lax.rem(c + 1 - step // half, 2)
    along = lax.rem(x + n_x - 1 - rest // inner, n_x)
    row = lax.rem(y + inner - 1 - lax.rem(rest, inner), inner)
    return core * half + along * inner + row


def coeff_kernel(
    sizes, total_rows, basis, image, chosen, out, shared, grams, got1, got2, got3, got4,
    send1, recv1, send2, recv2, send3, recv3, send4, recv4, csend, crecv
):
    n_rows, n_groups = sizes
    nsys = grams.shape[0]
    width = basis.shape[2]
    half, inner, n_x = nsys // 2, nsys // n_groups, n_groups // 2
    depth = n_rows // inner
    late = min(2, half - 1)
    step = pl.program_id(0)
    me_r = lax.axis_index("rows")
    me_g = lax.axis_index("groups")
    z, y, x, c = place_of(nsys, n_rows, n_groups)
    barrier = pltpu.get_barrier_semaphore()
    peers = n_rows * n_groups

    def at(t):
        return system_at(nsys, n_rows, n_groups, t)

    def nth_peer(i):
        other = lax.rem(me_r * n_groups + me_g + i, peers)
        return (other // n_groups, lax.rem(other, n_groups))

    def to_core(t):
        spot = lax.rem(at(t), half)
        return pltpu.make_async_remote_copy(
            src_ref=grams.at[at(t)],
            dst_ref=got1.at[spot],
            send_sem=send1.at[spot],
            recv_sem=recv1.at[spot],
            device_id=(me_r, me_g + 1 - 2 * c),
            device_id_type=MESH,
        )

    def along_x(dx, dy):
        spot = (dx - 1) * inner + lax.rem(y + dy, inner)
        k = lax.rem(x + dx, n_x)
        return pltpu.make_async_remote_copy(
            src_ref=grams.at[c * half + k * inner + lax.rem(y + dy, inner)],
            dst_ref=got2.at[spot],
            send_sem=send2.at[spot],
            recv_sem=recv2.at[spot],
            device_id=(me_r, k * 2 + c),
            device_id_type=MESH,
        )

    def along_rows(dy):
        k = lax.rem(y + dy, inner)
        return pltpu.make_async_remote_copy(
            src_ref=grams.at[c * half + x * inner + k],
            dst_ref=got3.at[dy - 1],
            send_sem=send3.at[dy - 1],
            recv_sem=recv3.at[dy - 1],
            device_id=(z * inner + k, me_g),
            device_id_type=MESH,
        )

    @pl.when(step == 0)
    def _():
        def greet(i, carry):
            pl.semaphore_signal(barrier, inc=1, device_id=nth_peer(i), device_id_type=MESH)
            return carry

        lax.fori_loop(1, peers, greet, 0)

    both = jnp.concatenate([basis[0], image[0]], axis=1)
    gram = lax.dot_general(both, both, TN, preferred_element_type=jnp.float32)
    cross, mixed, diag = pack(gram, width)
    now = at(step)
    grams[now, 0:width, :] = cross
    grams[now, width : 2 * width, :] = mixed
    grams[now, 2 * width :, :] = diag

    @pl.when(step == late)
    def _():
        pl.semaphore_wait(barrier, peers - 1)
        for t in range(late + 1):
            to_core(t).start()

    @pl.when(jnp.logical_and(step > late, step < half))
    def _():
        to_core(step).start()

    for t in range(half, nsys):

        @pl.when(step == t)
        def _():
            own = at(t)
            spot = lax.rem(own, half)
            to_core(t).wait_recv()
            grams[own] += got1[spot]
            dx = n_x - 1 - (t - half) // inner
            if dx:
                along_x(dx, inner - 1 - (t - half) % inner).start()

    @pl.when(step == nsys - 1)
    def _():
        base = c * half + x * inner
        for dy in reversed(range(inner)):
            k = lax.rem(y + dy, inner)
            for dx in range(1, n_x):
                along_x(dx, dy).wait_recv()
                grams[base + k] += got2[(dx - 1) * inner + k]
            if dy:
                along_rows(dy).start()
        mine = base + y
        for dy in range(1, inner):
            along_rows(dy).wait_recv()
            grams[mine] += got3[dy - 1]
        root = lax.rem(2 * c + x + y, depth)

        @pl.when(z != root)
        def _():
            copy = pltpu.make_async_remote_copy(
                src_ref=grams.at[mine],
                dst_ref=got4.at[lax.rem(z - root + depth, depth) - 1],
                send_sem=send4.at[0],
                recv_sem=recv4.at[lax.rem(z - root + depth, depth) - 1],
                device_id=(root * inner + y, me_g),
                device_id_type=MESH,
            )
            copy.start()
            copy.wait_send()

        @pl.when(z == root)
        def _():
            total = grams[mine]
            for k in range(depth - 1):
                pltpu.make_async_remote_copy(
                    src_ref=grams.at[mine],
                    dst_ref=got4.at[k],
                    send_sem=send4.at[0],
                    recv_sem=recv4.at[k],
                    device_id=(me_r, me_g),
                    device_id_type=MESH,
                ).wait_recv()
                total = total + got4[k]
            gram_s, cross_s, gram_f = unpack(total, width)
            picked = chosen[pl.ds(mine, 1), :]
            row = lax.broadcasted_iota(jnp.int32, (width, picked.shape[1]), 0)
            start = (row == picked).astype(jnp.float32).T
            coeffs = small_solve(gram_s, cross_s, gram_f, start, total_rows)
            shared[pl.ds(mine, 1)] = coeffs.astype(jnp.bfloat16)[None]

            def share(i):
                return pltpu.make_async_remote_copy(
                    src_ref=shared.at[mine],
                    dst_ref=shared.at[mine],
                    send_sem=csend.at[i],
                    recv_sem=crecv.at[mine],
                    device_id=nth_peer(i),
                    device_id_type=MESH,
                )

            def send(i, carry):
                share(i).start()
                return carry

            def sent(i, carry):
                share(i).wait_send()
                return carry

            lax.fori_loop(1, peers, send, 0)
            lax.fori_loop(1, peers, sent, 0)

        for s in range(nsys):

            @pl.when(jnp.logical_or(z != root, mine != s))
            def _():
                pltpu.make_async_remote_copy(
                    src_ref=shared.at[s],
                    dst_ref=shared.at[s],
                    send_sem=csend.at[0],
                    recv_sem=crecv.at[s],
                    device_id=(me_r, me_g),
                    device_id_type=MESH,
                ).wait_recv()

        for t in range(half):
            to_core(t).wait_send()
        for dy in range(inner):
            for dx in range(1, n_x):
                along_x(dx, dy).wait_send()
            if dy:
                along_rows(dy).wait_send()
        out[...] = shared[...]


def rotate_kernel(basis, image, coeffs, out):
    narrow = coeffs[0]
    empty = jnp.zeros_like(narrow)
    upper = jnp.concatenate([narrow, empty], axis=1)
    lower = jnp.concatenate([empty, narrow], axis=1)
    both = jnp.concatenate([basis[0], image[0]], axis=1)
    twice = jnp.concatenate([upper, lower], axis=0)
    turned = lax.dot_general(both, twice, NT, preferred_element_type=jnp.float32)
    out[0] = turned.astype(out.dtype)


def on_device(n_rows, n_groups, basis, image, selection):
    nsys, local, width = basis.shape
    keep = selection.shape[1]
    peers = n_rows * n_groups
    total_rows = local * peers
    inner = nsys // n_groups
    depth = n_rows // inner
    n_x = n_groups // 2
    tall = 2 * width + 8
    whole = pl.BlockSpec((1, local, width), lambda s: (s, 0, 0))
    ordered = pl.BlockSpec(
        (1, local, width), lambda s: (system_at(nsys, n_rows, n_groups, s), 0, 0)
    )
    coeffs = pl.pallas_call(
        functools.partial(coeff_kernel, (n_rows, n_groups), total_rows),
        grid=(nsys,),
        in_specs=[ordered, ordered, pl.BlockSpec(memory_space=pltpu.VMEM)],
        out_specs=pl.BlockSpec(memory_space=pltpu.VMEM),
        out_shape=jax.ShapeDtypeStruct((nsys, keep, width), jnp.bfloat16),
        scratch_shapes=[
            pltpu.VMEM((nsys, keep, width), jnp.bfloat16),
            pltpu.VMEM((nsys, tall, width), jnp.float32),
            pltpu.VMEM((nsys // 2, tall, width), jnp.float32),
            pltpu.VMEM(((n_x - 1) * nsys // n_groups, tall, width), jnp.float32),
            pltpu.VMEM((max(inner - 1, 1), tall, width), jnp.float32),
            pltpu.VMEM((depth - 1, tall, width), jnp.float32),
            pltpu.SemaphoreType.DMA((nsys // 2,)),
            pltpu.SemaphoreType.DMA((nsys // 2,)),
            pltpu.SemaphoreType.DMA(((n_x - 1) * inner,)),
            pltpu.SemaphoreType.DMA(((n_x - 1) * inner,)),
            pltpu.SemaphoreType.DMA((max(inner - 1, 1),)),
            pltpu.SemaphoreType.DMA((max(inner - 1, 1),)),
            pltpu.SemaphoreType.DMA((1,)),
            pltpu.SemaphoreType.DMA((depth - 1,)),
            pltpu.SemaphoreType.DMA((peers,)),
            pltpu.SemaphoreType.DMA((nsys,)),
        ],
        compiler_params=pltpu.CompilerParams(
            collective_id=0,
            has_side_effects=True,
            dimension_semantics=("arbitrary",),
            vmem_limit_bytes=16 << 20,
        ),
    )(basis, image, selection)
    return pl.pallas_call(
        rotate_kernel,
        grid=(nsys,),
        in_specs=[whole, whole, pl.BlockSpec((1, keep, width), lambda s: (s, 0, 0))],
        out_specs=whole,
        out_shape=jax.ShapeDtypeStruct((nsys, local, width), jnp.bfloat16),
        compiler_params=pltpu.CompilerParams(vmem_limit_bytes=16 << 20),
    )(basis, image, coeffs)


def solution(mesh):
    in_specs = (P(None, ("rows", "groups"), None), P(None, ("rows", "groups"), None), P())
    out_specs = P(None, ("rows", "groups"), None)
    return jax.shard_map(
        functools.partial(on_device, mesh.shape["rows"], mesh.shape["groups"]),
        mesh=mesh,
        in_specs=in_specs,
        out_specs=out_specs,
        check_vma=False,
    )
```

profile of v0, /device:TPU:0, one launch (start us, length us, event | category | flops | bytes accessed | tf_op | source)
XLA Modules:
  0.0 57.9 jit_solution(16506952536896377301)
XLA Ops:
  0.0 0.0 copy-start
  0.0 3.4 %copy-done = bf16[8,4096,128]{2,1,0:T(8,128)(2,1)S(1)} copy-done((bf16[8,4096,128]{2,1,0:T(8,128)(2,1)S(1)}, bf16[8,4096,128]{2,1,0:T(8,128)(2,1)}, u32[]{:S(2)}) %copy-start) | copy-done | bytes 8388632
  3.4 0.0 copy-start.1
  3.4 3.4 %copy-done.1 = bf16[8,4096,128]{2,1,0:T(8,128)(2,1)S(1)} copy-done((bf16[8,4096,128]{2,1,0:T(8,128)(2,1)S(1)}, bf16[8,4096,128]{2,1,0:T(8,128)(2,1)}, u32[]{:S(2)}) %copy-start.1) | copy-done | bytes 8388632
  6.8 0.0 copy-start.2
  6.8 0.7 %copy-done.2 = s32[8,64]{1,0:T(8,128)S(1)} copy-done((s32[8,64]{1,0:T(8,128)S(1)}, s32[8,64]{1,0:T(8,128)}, u32[]{:S(2)}) %copy-start.2) | copy-done | bytes 2072
  7.5 43.0 %shard_map.37.coeffs = bf16[8,64,128]{2,1,0:T(8,128)(2,1)S(1)} custom-call(bf16[8,4096,128]{2,1,0:T(8,128)(2,1)S(1)} %copy-done, bf16[8,4096,128]{2,1,0:T(8,128)(2,1)S(1)} %copy-done.1, s32[8,64]{1,0:T(8,128)S(1)} %copy-done.2), custom_call_target="tpu_custom_call" | custom-call | tf_op jit(solution)/shard_map/pallas_call | solution.py:350
  50.5 7.5 %shard_map.38 = bf16[8,4096,128]{2,1,0:T(8,128)(2,1)} custom-call(bf16[8,4096,128]{2,1,0:T(8,128)(2,1)S(1)} %copy-done, bf16[8,4096,128]{2,1,0:T(8,128)(2,1)S(1)} %copy-done.1, bf16[8,64,128]{2,1,0:T(8,128)(2,1)S(1)} %shard_map.37.coeffs), custom_call_target="tpu_custom_call" | custom-call | tf_op jit(solution)/shard_map/pallas_call | solution.py:381
Async XLA Ops:
  0.0 3.4 %copy-start = (bf16[8,4096,128]{2,1,0:T(8,128)(2,1)S(1)}, bf16[8,4096,128]{2,1,0:T(8,128)(2,1)}, u32[]{:S(2)}) copy-start(bf16[8,4096,128]{2,1,0:T(8,128)(2,1)} %basis.3) | copy-start | bytes 25165828
  3.4 3.4 %copy-start.1 = (bf16[8,4096,128]{2,1,0:T(8,128)(2,1)S(1)}, bf16[8,4096,128]{2,1,0:T(8,128)(2,1)}, u32[]{:S(2)}) copy-start(bf16[8,4096,128]{2,1,0:T(8,128)(2,1)} %image.3) | copy-start | bytes 25165828
  6.8 0.7 %copy-start.2 = (s32[8,64]{1,0:T(8,128)S(1)}, s32[8,64]{1,0:T(8,128)}, u32[]{:S(2)}) copy-start(s32[8,64]{1,0:T(8,128)} %chosen.1) | copy-start | bytes 6148
where the time goes:
time: 58.1 us; the launch traced here: 57.9 us
  Pallas kernels  50.5 us (87%)
  local copies, waits for them, and re-layouts  7.45 us (13%)
    pallas_call x1, Pallas kernels, on_device(): pl.pallas_call(functools.partial(coeff_kernel, (n_rows, n_groups), total_...  43 us
    pallas_call x1, Pallas kernels, on_device(): pl.pallas_call(rotate_kernel, grid=(nsys,), in_specs=[whole, whole, pl.Bl...  7.45 us
    unnamed x6, local copies, waits for them, and re-layouts  7.45 us

commit v1 on v0

v1 whole, which is shorter than its diff:
```python
import functools

import jax
import jax.numpy as jnp
from jax import lax
from jax.experimental import pallas as pl
from jax.experimental.pallas import tpu as pltpu
from jax.sharding import PartitionSpec as P

ITERS = 3
MESH = pl.DeviceIdType.MESH
NT = (((1,), (1,)), ((), ()))
TN = (((0,), (0,)), ((), ()))
HIGHEST = lax.Precision.HIGHEST


def exact_dot(a, b, dims=(((1,), (0,)), ((), ()))):
    return lax.dot_general(a, b, dims, precision=HIGHEST, preferred_element_type=jnp.float32)


def gram_of(a, b):
    return lax.dot_general(a, b, TN, preferred_element_type=jnp.float32)


def recip(x, refine):
    r = pl.reciprocal(x, approx=True)
    for _ in range(refine):
        r = r * (2.0 - x * r)
    return r


def row_of(tile, j):
    return jnp.broadcast_to(tile[j : j + 1, :], (8, 128))


def spread(tile, lane):
    return jnp.take_along_axis(tile, jnp.full((8, 128), lane, jnp.int32), axis=1)


def eliminate(cols, rest, refine):
    place = lax.broadcasted_iota(jnp.int32, (8, 128), 0)
    saved = []
    for j in range(0, 8, 2):
        c0, c1 = cols[j], cols[j + 1]
        a, b, d = row_of(c0, j), row_of(c1, j), row_of(c1, j + 1)
        det = a * d - b * b
        inv = recip(det, refine)
        ai, bi, di = a * inv, b * inv, d * inv
        first, second = place == j, place == j + 1

        def advance(v, urgent):
            v0, v1 = row_of(v, j), row_of(v, j + 1)
            if urgent:
                u0, u1 = (d * v0 - b * v1) * inv, (a * v1 - b * v0) * inv
            else:
                u0, u1 = di * v0 - bi * v1, ai * v1 - bi * v0
            new = v - c0 * u0 - c1 * u1
            return jnp.where(first, u0, jnp.where(second, u1, new))

        r0, r1 = row_of(rest, j), row_of(rest, j + 1)
        saved.append((r0, a * r1 - b * r0, a, det))
        for k in range(j + 2, len(cols)):
            cols[k] = advance(cols[k], k < j + 4)
        rest = advance(rest, False)
    return cols[8:], rest, saved


def rooted(saved, keep):
    place = lax.broadcasted_iota(jnp.int32, (8, 128), 0)
    tile = jnp.zeros((8, 128), jnp.float32)
    for q in range(4):
        v0, w1, a, det = saved[q]
        root = lax.rsqrt(a)
        tile = jnp.where(place == 2 * q, v0 * root, tile)
        tile = jnp.where(place == 2 * q + 1, w1 * (root * lax.rsqrt(det)), tile)
    return jnp.where(keep, tile, 0.0)


def less(tile, columns, rows):
    for c, r in zip(columns, rows):
        tile = tile - c * r
    return tile


def inverse_root(gram, refine=1):
    n = gram.shape[0]
    lane = lax.broadcasted_iota(jnp.int32, (8, 128), 1)
    place = lax.broadcasted_iota(jnp.int32, (8, 128), 0)
    tiles = [gram[8 * i : 8 * i + 8] for i in range(n // 8)]
    out = []
    for p in range(n // 16):
        first = 16 * p
        inside = jnp.logical_and(lane >= first, lane < first + 16)
        top, low = tiles[2 * p], tiles[2 * p + 1]
        top_cols = [spread(top, first + k) for k in range(16)]
        low_cols = [spread(low, first + k) for k in range(16)]
        far_cols = [[spread(x, first + k) for k in range(16)] for x in tiles[2 * p + 2 :]]
        top = jnp.where(inside, (lane - first == place).astype(jnp.float32), top)
        low = jnp.where(inside, (lane - first == place + 8).astype(jnp.float32), low)
        right, top, saved = eliminate(top_cols, top, refine)
        out.append(rooted(saved, lane < first + 8))
        rows = [row_of(top, k) for k in range(8)]
        low = less(low, low_cols[:8], rows)
        block = [less(low_cols[8 + k], low_cols[:8], [row_of(right[k], j) for j in range(8)]) for k in range(8)]
        _, low, saved = eliminate(block, low, refine)
        out.append(rooted(saved, lane < first + 16))
        rows = [row_of(low, k) for k in range(8)]
        top = less(top, right, rows)
        rows = [row_of(top, k) for k in range(8)] + rows
        for i, cols in enumerate(far_cols):
            j = 2 * p + 2 + i
            tiles[j] = less(jnp.where(inside, 0.0, tiles[j]), cols, rows)
    return jnp.concatenate(out, axis=0)


def padded(x):
    return jnp.concatenate([x, jnp.zeros_like(x)], axis=0)


def symmetric_pack(gram):
    half = gram.shape[0] // 2
    row = lax.broadcasted_iota(jnp.int32, (half, 2 * half), 0)
    lane = lax.broadcasted_iota(jnp.int32, (half, 2 * half), 1)
    low = pltpu.roll(gram[half:], half, 1)
    diag = jnp.sum(jnp.where(row == lane, low, 0.0), axis=0, keepdims=True)
    return jnp.where(lane < row, low, gram[:half]), jnp.broadcast_to(diag, (8, 2 * half))


def symmetric_unpack(packed):
    half = packed.shape[1] // 2
    mixed, diag = packed[:half], packed[half : half + 1]
    row = lax.broadcasted_iota(jnp.int32, (half, 2 * half), 0)
    lane = lax.broadcasted_iota(jnp.int32, (half, 2 * half), 1)
    turned = jnp.concatenate([mixed, jnp.zeros_like(mixed)], axis=0).T
    top = jnp.where(lane < row, turned[:half], mixed)
    low = jnp.where(lane < row, mixed, jnp.where(lane == row, diag, turned[:half]))
    low = jnp.where(lane < half, turned[half:], pltpu.roll(low, half, 1))
    return jnp.concatenate([top, low], axis=0)


def place_of(nsys, n_rows, n_groups):
    inner = nsys // n_groups
    me_r = lax.axis_index("rows")
    me_g = lax.axis_index("groups")
    return me_r // inner, lax.rem(me_r, inner), me_g // 2, lax.rem(me_g, 2)


def coeff_kernel(
    sizes, total_rows, basis, image, selection, held_w, held_q, out, shared, chosen,
    f_own, f_core, f_plane, f_deep, x_own, x_core, x_plane, x_deep, s_own, s_core, s_plane, s_deep,
    load_w, load_q, core_send, core_recv, plane_send, plane_recv, deep_send, deep_recv, csend, crecv, load_c
):
    n_rows, n_groups = sizes
    nsys, _, width = held_w.shape
    half, inner, n_x = nsys // 2, nsys // n_groups, n_groups // 2
    depth = n_rows // inner
    late = min(2, half - 1)
    me_r = lax.axis_index("rows")
    me_g = lax.axis_index("groups")
    z, y, x, c = place_of(nsys, n_rows, n_groups)
    barrier = pltpu.get_barrier_semaphore()
    peers = n_rows * n_groups
    mine = c * half + x * inner + y
    root = lax.rem((depth - 1) // 2 + lax.rem(c + x + y, 2), depth)
    kinds = ((f_own, f_core, f_plane, f_deep), (x_own, x_core, x_plane, x_deep), (s_own, s_core, s_plane, s_deep))

    def at(t):
        rest = lax.rem(t, half)
        core = lax.rem(c + 1 - t // half, 2)
        along = lax.rem(x + n_x - 1 - rest // inner, n_x)
        return core * half + along * inner + lax.rem(y + inner - 1 - lax.rem(rest, inner), inner)

    def nth_peer(i):
        other = lax.rem(me_r * n_groups + me_g + i, peers)
        return (other // n_groups, lax.rem(other, n_groups))

    def load(source, target, sems, s):
        return pltpu.make_async_copy(source.at[s], target.at[s], sems.at[s])

    def to_core(kind, s):
        own, got = kinds[kind][0], kinds[kind][1]
        spot = lax.rem(s, half)
        return pltpu.make_async_remote_copy(
            src_ref=own.at[s],
            dst_ref=got.at[spot],
            send_sem=core_send.at[kind, spot],
            recv_sem=core_recv.at[kind, spot],
            device_id=(me_r, me_g + 1 - 2 * c),
            device_id_type=MESH,
        )

    def in_plane(kind, rest):
        own, got = kinds[kind][0], kinds[kind][2]
        k = lax.rem(x + n_x - 1 - rest // inner, n_x)
        j = lax.rem(y + inner - 1 - lax.rem(rest, inner), inner)
        return pltpu.make_async_remote_copy(
            src_ref=own.at[c * half + k * inner + j],
            dst_ref=got.at[rest],
            send_sem=plane_send.at[kind, rest],
            recv_sem=plane_recv.at[kind, rest],
            device_id=(z * inner + j, k * 2 + c),
            device_id_type=MESH,
        )

    def to_root(kind):
        own, got = kinds[kind][0], kinds[kind][3]
        spot = lax.rem(z - root + depth, depth) - 1
        return pltpu.make_async_remote_copy(
            src_ref=own.at[mine],
            dst_ref=got.at[spot],
            send_sem=deep_send.at[kind],
            recv_sem=deep_recv.at[kind, spot],
            device_id=(root * inner + y, me_g),
            device_id_type=MESH,
        )

    def from_depth(kind, i):
        own, got = kinds[kind][0], kinds[kind][3]
        return pltpu.make_async_remote_copy(
            src_ref=own.at[mine],
            dst_ref=got.at[i],
            send_sem=deep_send.at[kind],
            recv_sem=deep_recv.at[kind, i],
            device_id=(me_r, me_g),
            device_id_type=MESH,
        )

    def plane_sum(kind):
        own, got = kinds[kind][0], kinds[kind][2]
        total = own[mine]
        for rest in range(half - 1):
            in_plane(kind, rest).wait_recv()
            total = total + got[rest]
        return total

    def root_sum(kind):
        total = plane_sum(kind)
        for i in range(depth - 1):
            from_depth(kind, i).wait_recv()
            total = total + kinds[kind][3][i]
        return total

    def first_load(t, carry):
        load(image, held_q, load_q, at(t)).start()
        return carry

    def second_load(t, carry):
        load(basis, held_w, load_w, at(t)).start()
        return carry

    lax.fori_loop(0, nsys, first_load, 0)
    lax.fori_loop(0, nsys, second_load, 0)
    pltpu.make_async_copy(selection, chosen, load_c.at[0]).start()

    def greet(i, carry):
        pl.semaphore_signal(barrier, inc=1, device_id=nth_peer(i), device_id_type=MESH)
        return carry

    lax.fori_loop(1, peers, greet, 0)

    def first_gram(t, carry):
        s = at(t)
        load(image, held_q, load_q, s).wait()
        right = held_q[s]
        mixed, diag = symmetric_pack(gram_of(right, right))
        f_own[s, 0 : width // 2, :] = mixed
        f_own[s, width // 2 :, :] = diag

        @pl.when(t == late)
        def _():
            pl.semaphore_wait(barrier, peers - 1)
            for u in range(late + 1):
                to_core(0, at(u)).start()

        @pl.when(jnp.logical_and(t > late, t < half))
        def _():
            to_core(0, s).start()

        @pl.when(t >= half)
        def _():
            to_core(0, s).wait_recv()
            f_own[s] += f_core[lax.rem(s, half)]

            @pl.when(t < nsys - 1)
            def _():
                in_plane(0, t - half).start()

        return carry

    lax.fori_loop(0, nsys, first_gram, 0)

    def second_gram(t, carry):
        s = at(t)
        load(basis, held_w, load_w, s).wait()
        left = held_w[s]
        pair = gram_of(left, jnp.concatenate([left, held_q[s]], axis=1))
        mixed, diag = symmetric_pack(pair[:, :width])
        s_own[s, 0 : width // 2, :] = mixed
        s_own[s, width // 2 :, :] = diag
        x_own[s] = pair[:, width:]

        @pl.when(t < half)
        def _():
            to_core(1, s).start()
            to_core(2, s).start()

        @pl.when(t >= half)
        def _():
            to_core(1, s).wait_recv()
            x_own[s] += x_core[lax.rem(s, half)]

            @pl.when(t < nsys - 1)
            def _():
                in_plane(1, t - half).start()

            to_core(2, s).wait_recv()
            s_own[s] += s_core[lax.rem(s, half)]

        return carry

    lax.fori_loop(0, nsys, second_gram, 0)

    for rest in range(half - 1):
        in_plane(2, rest).start()
    pltpu.make_async_copy(selection, chosen, load_c.at[0]).wait()

    @pl.when(z != root)
    def _():
        for kind in range(3):
            kinds[kind][0][mine] = plane_sum(kind)
            to_root(kind).start()
        for kind in range(3):
            to_root(kind).wait_send()

    @pl.when(z == root)
    def _():
        half_inverse = inverse_root(symmetric_unpack(root_sum(0)))
        across = exact_dot(exact_dot(root_sum(1), half_inverse, NT), half_inverse)
        gram_s = symmetric_unpack(root_sum(2))
        both = jnp.concatenate([across, exact_dot(across, gram_s)], axis=1)
        picked = chosen[pl.ds(mine, 1), :]
        row = lax.broadcasted_iota(jnp.int32, (width, picked.shape[1]), 0)
        now = exact_dot((row == picked).astype(jnp.float32).T, both)
        for step in range(ITERS):
            solved = now[:, :width]
            last = step == ITERS - 1
            weighted = exact_dot(solved, gram_s) if last else now[:, width:]
            metric = exact_dot(solved, padded(weighted), NT) * (1.0 / total_rows)
            lower = inverse_root(metric, 1 if last else 0)
            now = exact_dot(lower, padded(solved if last else exact_dot(solved, both)))
        shared[pl.ds(mine, 1)] = now.astype(jnp.bfloat16)[None]

        def share(i):
            return pltpu.make_async_remote_copy(
                src_ref=shared.at[mine],
                dst_ref=shared.at[mine],
                send_sem=csend.at[i],
                recv_sem=crecv.at[mine],
                device_id=nth_peer(i),
                device_id_type=MESH,
            )

        def send(i, carry):
            share(i).start()
            return carry

        def sent(i, carry):
            share(i).wait_send()
            return carry

        lax.fori_loop(1, peers, send, 0)
        lax.fori_loop(1, peers, sent, 0)

    for s in range(nsys):

        @pl.when(jnp.logical_or(z != root, mine != s))
        def _():
            pltpu.make_async_remote_copy(
                src_ref=shared.at[s],
                dst_ref=shared.at[s],
                send_sem=csend.at[0],
                recv_sem=crecv.at[s],
                device_id=(me_r, me_g),
                device_id_type=MESH,
            ).wait_recv()

    for kind in range(3):
        for t in range(half):
            to_core(kind, at(t)).wait_send()
        for rest in range(half - 1):
            in_plane(kind, rest).wait_send()
    out[...] = shared[...]


def rotate_kernel(basis, image, coeffs, out):
    narrow = coeffs[0]
    empty = jnp.zeros_like(narrow)
    upper = jnp.concatenate([narrow, empty], axis=1)
    lower = jnp.concatenate([empty, narrow], axis=1)
    both = jnp.concatenate([basis[0], image[0]], axis=1)
    twice = jnp.concatenate([upper, lower], axis=0)
    turned = lax.dot_general(both, twice, NT, preferred_element_type=jnp.float32)
    out[0] = turned.astype(out.dtype)


def on_device(n_rows, n_groups, basis, image, selection):
    nsys, local, width = basis.shape
    keep = selection.shape[1]
    peers = n_rows * n_groups
    total_rows = local * peers
    half, inner = nsys // 2, nsys // n_groups
    depth = n_rows // inner
    near, far = max(half - 1, 1), max(depth - 1, 1)
    packed = width // 2 + 8
    in_hbm = pl.BlockSpec(memory_space=pltpu.HBM)
    in_vmem = pl.BlockSpec(memory_space=pltpu.VMEM)
    held = jax.ShapeDtypeStruct((nsys, local, width), jnp.bfloat16)
    buffers = [
        pltpu.VMEM((count, tall, width), jnp.float32)
        for tall in (packed, width, packed)
        for count in (nsys, half, near, far)
    ]
    held_w, held_q, coeffs = pl.pallas_call(
        functools.partial(coeff_kernel, (n_rows, n_groups), total_rows),
        in_specs=[in_hbm, in_hbm, in_hbm],
        out_specs=[in_vmem, in_vmem, in_vmem],
        out_shape=[held, held, jax.ShapeDtypeStruct((nsys, keep, width), jnp.bfloat16)],
        scratch_shapes=[
            pltpu.VMEM((nsys, keep, width), jnp.bfloat16),
            pltpu.VMEM((nsys, keep), jnp.int32),
            *buffers,
            pltpu.SemaphoreType.DMA((nsys,)),
            pltpu.SemaphoreType.DMA((nsys,)),
            pltpu.SemaphoreType.DMA((3, half)),
            pltpu.SemaphoreType.DMA((3, half)),
            pltpu.SemaphoreType.DMA((3, near)),
            pltpu.SemaphoreType.DMA((3, near)),
            pltpu.SemaphoreType.DMA((3,)),
            pltpu.SemaphoreType.DMA((3, far)),
            pltpu.SemaphoreType.DMA((peers,)),
            pltpu.SemaphoreType.DMA((nsys,)),
            pltpu.SemaphoreType.DMA((1,)),
        ],
        compiler_params=pltpu.CompilerParams(
            collective_id=0,
            has_side_effects=True,
            vmem_limit_bytes=16 << 20,
        ),
    )(*(pltpu.with_memory_space_constraint(v, pltpu.HBM) for v in (basis, image, selection)))
    whole = pl.BlockSpec((1, local, width), lambda s: (s, 0, 0))
    return pl.pallas_call(
        rotate_kernel,
        grid=(nsys,),
        in_specs=[whole, whole, pl.BlockSpec((1, keep, width), lambda s: (s, 0, 0))],
        out_specs=whole,
        out_shape=jax.ShapeDtypeStruct((nsys, local, width), jnp.bfloat16),
        compiler_params=pltpu.CompilerParams(vmem_limit_bytes=16 << 20),
    )(held_w, held_q, coeffs)


def solution(mesh):
    in_specs = (P(None, ("rows", "groups"), None), P(None, ("rows", "groups"), None), P())
    out_specs = P(None, ("rows", "groups"), None)
    return jax.shard_map(
        functools.partial(on_device, mesh.shape["rows"], mesh.shape["groups"]),
        mesh=mesh,
        in_specs=in_specs,
        out_specs=out_specs,
        check_vma=False,
    )
```

time: 58.1 us -> 42.3 us (0.73)
  Pallas kernels: 50.5 us -> 42.1 us
  local copies, waits for them, and re-layouts: 7.45 us -> 0 us
    pallas_call x1, Pallas kernels: 43 us -> 34.7 us  [on_device(): pl.pallas_call(functools.partial(coeff_kernel, (n_rows, n_groups), total_...]
    unnamed x6 -> x0, local copies, waits for them, and re-layouts: 7.45 us -> none
where the time goes in v1:
time: 42.3 us; the launch traced here: 42.2 us
  Pallas kernels  42.1 us (100%)
    pallas_call x1, Pallas kernels, on_device(): pl.pallas_call(functools.partial(coeff_kernel, (n_rows, n_groups), total_...  34.7 us
    pallas_call x1, Pallas kernels, on_device(): pl.pallas_call(rotate_kernel, grid=(nsys,), in_specs=[whole, whole, pl.Bl...  7.45 us

profile of v1, /device:TPU:0, one launch (start us, length us, event | category | flops | bytes accessed | tf_op | source)
XLA Modules:
  0.0 42.2 jit_solution(8435768740421851966)
XLA Ops:
  0.0 34.7 %shard_map.37 = (bf16[8,4096,128]{2,1,0:T(8,128)(2,1)S(1)}, bf16[8,4096,128]{2,1,0:T(8,128)(2,1)S(1)}, bf16[8,64,128]{2,1,0:T(8,128)(2,1)S(1)}) custom-call(bf16[8,4096,128]{2,1,0:T(8,128)(2,1)} %basis.1, bf16[8,4096,128]{2,1,0:T(8,128)(2,1)} %image.1, s32[8,64]{1,0:T(8,128)} %selection.1), custom_call_target="tpu_custom_call" | custom-call | tf_op jit(solution)/shard_map/pallas_call | solution.py:423
  34.7 7.5 %shard_map.38 = bf16[8,4096,128]{2,1,0:T(8,128)(2,1)} custom-call(bf16[8,4096,128]{2,1,0:T(8,128)(2,1)S(1)} %get-tuple-element.8.basis, bf16[8,4096,128]{2,1,0:T(8,128)(2,1)S(1)} %get-tuple-element.9.image, bf16[8,64,128]{2,1,0:T(8,128)(2,1)S(1)} %get-tuple-element.10.coeffs), custom_call_target="tpu_custom_call" | custom-call | tf_op jit(solution)/shard_map/pallas_call | solution.py:451

commit v2 on v1

--- a/solution.py
+++ b/solution.py
@@ -8,6 +8,9 @@
 from jax.sharding import PartitionSpec as P
 
 ITERS = 3
+BATCH = 4
+LATE = 0
+AHEAD = 3
 MESH = pl.DeviceIdType.MESH
 NT = (((1,), (1,)), ((), ()))
 TN = (((0,), (0,)), ((), ()))
@@ -82,12 +85,11 @@
     return tile
 
 
-def inverse_root(gram, refine=1):
+def inverse_root_tiles(gram, refine=1):
     n = gram.shape[0]
     lane = lax.broadcasted_iota(jnp.int32, (8, 128), 1)
     place = lax.broadcasted_iota(jnp.int32, (8, 128), 0)
     tiles = [gram[8 * i : 8 * i + 8] for i in range(n // 8)]
-    out = []
     for p in range(n // 16):
         first = 16 * p
         inside = jnp.logical_and(lane >= first, lane < first + 16)
@@ -98,19 +100,22 @@
         top = jnp.where(inside, (lane - first == place).astype(jnp.float32), top)
         low = jnp.where(inside, (lane - first == place + 8).astype(jnp.float32), low)
         right, top, saved = eliminate(top_cols, top, refine)
-        out.append(rooted(saved, lane < first + 8))
+        upper = rooted(saved, lane < first + 8)
         rows = [row_of(top, k) for k in range(8)]
         low = less(low, low_cols[:8], rows)
         block = [less(low_cols[8 + k], low_cols[:8], [row_of(right[k], j) for j in range(8)]) for k in range(8)]
         _, low, saved = eliminate(block, low, refine)
-        out.append(rooted(saved, lane < first + 16))
+        yield upper, rooted(saved, lane < first + 16)
         rows = [row_of(low, k) for k in range(8)]
         top = less(top, right, rows)
         rows = [row_of(top, k) for k in range(8)] + rows
         for i, cols in enumerate(far_cols):
             j = 2 * p + 2 + i
             tiles[j] = less(jnp.where(inside, 0.0, tiles[j]), cols, rows)
-    return jnp.concatenate(out, axis=0)
+
+
+def inverse_root(gram, refine=1):
+    return jnp.concatenate([x for pair in inverse_root_tiles(gram, refine) for x in pair], axis=0)
 
 
 def padded(x):
@@ -124,6 +129,13 @@
     low = pltpu.roll(gram[half:], half, 1)
     diag = jnp.sum(jnp.where(row == lane, low, 0.0), axis=0, keepdims=True)
     return jnp.where(lane < row, low, gram[:half]), jnp.broadcast_to(diag, (8, 2 * half))
+
+
+def diagonal_row(gram):
+    row = lax.broadcasted_iota(jnp.int32, gram.shape, 0)
+    lane = lax.broadcasted_iota(jnp.int32, gram.shape, 1)
+    diag = jnp.sum(jnp.where(row == lane, gram, 0.0), axis=0, keepdims=True)
+    return jnp.broadcast_to(diag, (8, gram.shape[1]))
 
 
 def symmetric_unpack(packed):
@@ -147,14 +159,17 @@
 
 def coeff_kernel(
     sizes, total_rows, basis, image, selection, held_w, held_q, out, shared, chosen,
-    f_own, f_core, f_plane, f_deep, x_own, x_core, x_plane, x_deep, s_own, s_core, s_plane, s_deep,
+    f_own, f_core, f_plane, f_deep, x_top, x_top_core, x_top_plane, x_top_deep,
+    x_low, x_low_core, x_low_plane, x_low_deep, s_own, s_core, s_plane, s_deep,
     load_w, load_q, core_send, core_recv, plane_send, plane_recv, deep_send, deep_recv, csend, crecv, load_c
 ):
     n_rows, n_groups = sizes
     nsys, _, width = held_w.shape
     half, inner, n_x = nsys // 2, nsys // n_groups, n_groups // 2
     depth = n_rows // inner
-    late = min(2, half - 1)
+    batch = BATCH if half % BATCH == 0 else 1
+    groups = nsys // batch
+    late = min(LATE, groups // 2 - 1)
     me_r = lax.axis_index("rows")
     me_g = lax.axis_index("groups")
     z, y, x, c = place_of(nsys, n_rows, n_groups)
@@ -162,7 +177,12 @@
     peers = n_rows * n_groups
     mine = c * half + x * inner + y
     root = lax.rem((depth - 1) // 2 + lax.rem(c + x + y, 2), depth)
-    kinds = ((f_own, f_core, f_plane, f_deep), (x_own, x_core, x_plane, x_deep), (s_own, s_core, s_plane, s_deep))
+    kinds = (
+        (f_own, f_core, f_plane, f_deep),
+        (x_top, x_top_core, x_top_plane, x_top_deep),
+        (x_low, x_low_core, x_low_plane, x_low_deep),
+        (s_own, s_core, s_plane, s_deep),
+    )
 
     def at(t):
         rest = lax.rem(t, half)
@@ -225,6 +245,16 @@
             device_id_type=MESH,
         )
 
+    def arrived(s):
+        return pltpu.make_async_remote_copy(
+            src_ref=shared.at[s],
+            dst_ref=shared.at[s],
+            send_sem=csend.at[0],
+            recv_sem=crecv.at[s],
+            device_id=(me_r, me_g),
+            device_id_type=MESH,
+        )
+
     def plane_sum(kind):
         own, got = kinds[kind][0], kinds[kind][2]
         total = own[mine]
@@ -240,16 +270,15 @@
             total = total + kinds[kind][3][i]
         return total
 
-    def first_load(t, carry):
-        load(image, held_q, load_q, at(t)).start()
-        return carry
-
-    def second_load(t, carry):
-        load(basis, held_w, load_w, at(t)).start()
-        return carry
-
-    lax.fori_loop(0, nsys, first_load, 0)
-    lax.fori_loop(0, nsys, second_load, 0)
+    def start_load(g):
+        for u in range(batch):
+            if g < groups:
+                load(image, held_q, load_q, at(g * batch + u)).start()
+            else:
+                load(basis, held_w, load_w, at((g - groups) * batch + u)).start()
+
+    for g in range(AHEAD):
+        start_load(g)
     pltpu.make_async_copy(selection, chosen, load_c.at[0]).start()
 
     def greet(i, carry):
@@ -258,133 +287,136 @@
 
     lax.fori_loop(1, peers, greet, 0)
 
-    def first_gram(t, carry):
-        s = at(t)
-        load(image, held_q, load_q, s).wait()
-        right = held_q[s]
-        mixed, diag = symmetric_pack(gram_of(right, right))
-        f_own[s, 0 : width // 2, :] = mixed
-        f_own[s, width // 2 :, :] = diag
-
-        @pl.when(t == late)
-        def _():
+    def issue(g):
+        if g + AHEAD < 2 * groups:
+            start_load(g + AHEAD)
+
+    def first_gram(g):
+        spots = [at(g * batch + u) for u in range(batch)]
+        pieces = [spots[:2], spots[2:]] if g == 0 else [spots]
+        for piece in pieces:
+            for s in piece:
+                load(image, held_q, load_q, s).wait()
+            if piece is pieces[-1]:
+                issue(g)
+            for s in piece:
+                right = held_q[s]
+                mixed, diag = symmetric_pack(gram_of(right, right))
+                f_own[s, 0 : width // 2, :] = mixed
+                f_own[s, width // 2 :, :] = diag
+        if g == late:
             pl.semaphore_wait(barrier, peers - 1)
-            for u in range(late + 1):
-                to_core(0, at(u)).start()
-
-        @pl.when(jnp.logical_and(t > late, t < half))
-        def _():
-            to_core(0, s).start()
-
-        @pl.when(t >= half)
-        def _():
-            to_core(0, s).wait_recv()
-            f_own[s] += f_core[lax.rem(s, half)]
-
-            @pl.when(t < nsys - 1)
-            def _():
-                in_plane(0, t - half).start()
-
-        return carry
-
-    lax.fori_loop(0, nsys, first_gram, 0)
-
-    def second_gram(t, carry):
-        s = at(t)
-        load(basis, held_w, load_w, s).wait()
-        left = held_w[s]
-        pair = gram_of(left, jnp.concatenate([left, held_q[s]], axis=1))
-        mixed, diag = symmetric_pack(pair[:, :width])
-        s_own[s, 0 : width // 2, :] = mixed
-        s_own[s, width // 2 :, :] = diag
-        x_own[s] = pair[:, width:]
-
-        @pl.when(t < half)
-        def _():
-            to_core(1, s).start()
-            to_core(2, s).start()
-
-        @pl.when(t >= half)
-        def _():
-            to_core(1, s).wait_recv()
-            x_own[s] += x_core[lax.rem(s, half)]
-
-            @pl.when(t < nsys - 1)
-            def _():
-                in_plane(1, t - half).start()
-
-            to_core(2, s).wait_recv()
-            s_own[s] += s_core[lax.rem(s, half)]
-
-        return carry
-
-    lax.fori_loop(0, nsys, second_gram, 0)
-
-    for rest in range(half - 1):
-        in_plane(2, rest).start()
+            for t in range((late + 1) * batch):
+                to_core(0, at(t)).start()
+        elif late < g < groups // 2:
+            for s in spots:
+                to_core(0, s).start()
+        if g >= groups // 2:
+            for u, s in enumerate(spots):
+                to_core(0, s).wait_recv()
+                f_own[s] += f_core[lax.rem(s, half)]
+                if g * batch + u < nsys - 1:
+                    in_plane(0, g * batch + u - half).start()
+
+    def second_gram(g):
+        spots = [at(g * batch + u) for u in range(batch)]
+        for s in spots:
+            load(basis, held_w, load_w, s).wait()
+        issue(g + groups)
+        for s in spots:
+            left = held_w[s]
+            pair = gram_of(left, jnp.concatenate([left, held_q[s]], axis=1))
+            mixed, diag = symmetric_pack(pair[:, :width])
+            s_own[s, 0 : width // 2, :] = mixed
+            s_own[s, width // 2 :, :] = diag
+            x_top[s] = pair[: width // 2, width:]
+            x_low[s, 0 : width // 2, :] = pair[width // 2 :, width:]
+            x_low[s, width // 2 :, :] = diagonal_row(pair[:, :width])
+        if g < groups // 2:
+            for s in spots:
+                for kind in (1, 2, 3):
+                    to_core(kind, s).start()
+        else:
+            for kind in (1, 2):
+                for u, s in enumerate(spots):
+                    own, got = kinds[kind][0], kinds[kind][1]
+                    to_core(kind, s).wait_recv()
+                    own[s] += got[lax.rem(s, half)]
+                    if g * batch + u < nsys - 1:
+                        in_plane(kind, g * batch + u - half).start()
+            for u, s in enumerate(spots):
+                to_core(3, s).wait_recv()
+                s_own[s] += s_core[lax.rem(s, half)]
+                if g * batch + u < nsys - 1:
+                    in_plane(3, g * batch + u - half).start()
+
+    for g in range(groups):
+        first_gram(g)
+    for g in range(groups):
+        second_gram(g)
     pltpu.make_async_copy(selection, chosen, load_c.at[0]).wait()
 
     @pl.when(z != root)
     def _():
-        for kind in range(3):
+        for kind in range(4):
             kinds[kind][0][mine] = plane_sum(kind)
             to_root(kind).start()
-        for kind in range(3):
+        for kind in range(4):
             to_root(kind).wait_send()
 
     @pl.when(z == root)
     def _():
         half_inverse = inverse_root(symmetric_unpack(root_sum(0)))
-        across = exact_dot(exact_dot(root_sum(1), half_inverse, NT), half_inverse)
-        gram_s = symmetric_unpack(root_sum(2))
-        both = jnp.concatenate([across, exact_dot(across, gram_s)], axis=1)
+        inverse = exact_dot(half_inverse, half_inverse, TN)
+        low = root_sum(2)
+        across = exact_dot(jnp.concatenate([root_sum(1), low[: width // 2]], axis=0), inverse)
+        weight = jnp.broadcast_to(low[width // 2 : width // 2 + 1], (selection.shape[1], width))
         picked = chosen[pl.ds(mine, 1), :]
         row = lax.broadcasted_iota(jnp.int32, (width, picked.shape[1]), 0)
-        now = exact_dot((row == picked).astype(jnp.float32).T, both)
-        for step in range(ITERS):
-            solved = now[:, :width]
-            last = step == ITERS - 1
-            weighted = exact_dot(solved, gram_s) if last else now[:, width:]
-            metric = exact_dot(solved, padded(weighted), NT) * (1.0 / total_rows)
-            lower = inverse_root(metric, 1 if last else 0)
-            now = exact_dot(lower, padded(solved if last else exact_dot(solved, both)))
+        solved = exact_dot((row == picked).astype(jnp.float32).T, across)
+        for step in range(ITERS - 1):
+            metric = exact_dot(solved, padded(solved * weight), NT)
+            solved = exact_dot(inverse_root(metric, 0), padded(exact_dot(solved, across)))
+        gram_s = symmetric_unpack(root_sum(3))
+        metric = exact_dot(solved, padded(exact_dot(solved, gram_s)), NT) * (1.0 / total_rows)
+        now = exact_dot(inverse_root(metric), padded(solved))
         shared[pl.ds(mine, 1)] = now.astype(jnp.bfloat16)[None]
 
-        def share(i):
+        def share(i, far, dx, dy, dc):
+            to_row = lax.rem(z + far, depth) * inner + lax.rem(y + dy, inner)
             return pltpu.make_async_remote_copy(
                 src_ref=shared.at[mine],
                 dst_ref=shared.at[mine],
                 send_sem=csend.at[i],
                 recv_sem=crecv.at[mine],
-                device_id=nth_peer(i),
+                device_id=(to_row, lax.rem(x + dx, n_x) * 2 + lax.rem(c + dc, 2)),
                 device_id_type=MESH,
             )
 
-        def send(i, carry):
-            share(i).start()
-            return carry
-
-        def sent(i, carry):
-            share(i).wait_send()
-            return carry
-
-        lax.fori_loop(1, peers, send, 0)
-        lax.fori_loop(1, peers, sent, 0)
+        def steps(o, n):
+            return min(o, n - o)
+
+        spots = [
+            (far, dx, dy, dc)
+            for far in range(depth)
+            for dx in range(n_x)
+            for dy in range(inner)
+            for dc in range(2)
+        ][1:]
+        spots.sort(key=lambda v: -(steps(v[0], depth) + steps(v[1], n_x) + steps(v[2], inner)))
+
+        for i, spot in enumerate(spots):
+            share(i, *spot).start()
+        for i, spot in enumerate(spots):
+            share(i, *spot).wait_send()
 
     for s in range(nsys):
 
         @pl.when(jnp.logical_or(z != root, mine != s))
         def _():
-            pltpu.make_async_remote_copy(
-                src_ref=shared.at[s],
-                dst_ref=shared.at[s],
-                send_sem=csend.at[0],
-                recv_sem=crecv.at[s],
-                device_id=(me_r, me_g),
-                device_id_type=MESH,
-            ).wait_recv()
-
-    for kind in range(3):
+            arrived(s).wait_recv()
+
+    for kind in range(4):
         for t in range(half):
             to_core(kind, at(t)).wait_send()
         for rest in range(half - 1):
@@ -392,15 +424,19 @@
     out[...] = shared[...]
 
 
-def rotate_kernel(basis, image, coeffs, out):
-    narrow = coeffs[0]
-    empty = jnp.zeros_like(narrow)
-    upper = jnp.concatenate([narrow, empty], axis=1)
-    lower = jnp.concatenate([empty, narrow], axis=1)
-    both = jnp.concatenate([basis[0], image[0]], axis=1)
-    twice = jnp.concatenate([upper, lower], axis=0)
-    turned = lax.dot_general(both, twice, NT, preferred_element_type=jnp.float32)
-    out[0] = turned.astype(out.dtype)
+def rotate_kernel(basis, image, coeffs, out, ready, sems):
+    def store(s):
+        return pltpu.make_async_copy(ready.at[s], out.at[s], sems.at[s])
+
+    nsys = basis.shape[0]
+    for s in range(nsys):
+        narrow = coeffs[s]
+        left = lax.dot_general(basis[s], narrow, NT, preferred_element_type=jnp.float32)
+        right = lax.dot_general(image[s], narrow, NT, preferred_element_type=jnp.float32)
+        ready[s] = jnp.concatenate([left, right], axis=1).astype(out.dtype)
+        store(s).start()
+    for s in range(nsys):
+        store(s).wait()
 
 
 def on_device(n_rows, n_groups, basis, image, selection):
@@ -417,7 +453,7 @@
     held = jax.ShapeDtypeStruct((nsys, local, width), jnp.bfloat16)
     buffers = [
         pltpu.VMEM((count, tall, width), jnp.float32)
-        for tall in (packed, width, packed)
+        for tall in (packed, width // 2, packed, packed)
         for count in (nsys, half, near, far)
     ]
     held_w, held_q, coeffs = pl.pallas_call(
@@ -431,12 +467,12 @@
             *buffers,
             pltpu.SemaphoreType.DMA((nsys,)),
             pltpu.SemaphoreType.DMA((nsys,)),
-            pltpu.SemaphoreType.DMA((3, half)),
-            pltpu.SemaphoreType.DMA((3, half)),
-            pltpu.SemaphoreType.DMA((3, near)),
-            pltpu.SemaphoreType.DMA((3, near)),
-            pltpu.SemaphoreType.DMA((3,)),
-            pltpu.SemaphoreType.DMA((3, far)),
+            pltpu.SemaphoreType.DMA((4, half)),
+            pltpu.SemaphoreType.DMA((4, half)),
+            pltpu.SemaphoreType.DMA((4, near)),
+            pltpu.SemaphoreType.DMA((4, near)),
+            pltpu.SemaphoreType.DMA((4,)),
+            pltpu.SemaphoreType.DMA((4, far)),
             pltpu.SemaphoreType.DMA((peers,)),
             pltpu.SemaphoreType.DMA((nsys,)),
             pltpu.SemaphoreType.DMA((1,)),
@@ -447,13 +483,12 @@
             vmem_limit_bytes=16 << 20,
         ),
     )(*(pltpu.with_memory_space_constraint(v, pltpu.HBM) for v in (basis, image, selection)))
-    whole = pl.BlockSpec((1, local, width), lambda s: (s, 0, 0))
     return pl.pallas_call(
         rotate_kernel,
-        grid=(nsys,),
-        in_specs=[whole, whole, pl.BlockSpec((1, keep, width), lambda s: (s, 0, 0))],
-        out_specs=whole,
-        out_shape=jax.ShapeDtypeStruct((nsys, local, width), jnp.bfloat16),
+        in_specs=[in_vmem, in_vmem, in_vmem],
+        out_specs=in_hbm,
+        out_shape=held,
+        scratch_shapes=[pltpu.VMEM((nsys, local, width), jnp.bfloat16), pltpu.SemaphoreType.DMA((nsys,))],
         compiler_params=pltpu.CompilerParams(vmem_limit_bytes=16 << 20),
     )(held_w, held_q, coeffs)
 

time: 42.3 us -> 38.7 us (0.915)
  Pallas kernels: 42.1 us -> 38.4 us
    pallas_call x1, Pallas kernels: 34.7 us -> 32.7 us  [on_device(): pl.pallas_call(functools.partial(coeff_kernel, (n_rows, n_groups), total_...]
    pallas_call x1, Pallas kernels: 7.45 us -> 5.62 us  [on_device(): pl.pallas_call(rotate_kernel, in_specs=[in_vmem, in_vmem, in_vmem], out_s...]
where the time goes in v2:
time: 38.7 us; the launch traced here: 38.6 us
  Pallas kernels  38.4 us (99%)
    pallas_call x1, Pallas kernels, on_device(): pl.pallas_call(functools.partial(coeff_kernel, (n_rows, n_groups), total_...  32.7 us
    pallas_call x1, Pallas kernels, on_device(): pl.pallas_call(rotate_kernel, in_specs=[in_vmem, in_vmem, in_vmem], out_s...  5.62 us

profile of v2, /device:TPU:0, one launch (start us, length us, event | category | flops | bytes accessed | tf_op | source)
XLA Modules:
  0.0 38.6 jit_solution(6990746182608561334)
XLA Ops:
  0.0 32.7 %shard_map.37 = (bf16[8,4096,128]{2,1,0:T(8,128)(2,1)S(1)}, bf16[8,4096,128]{2,1,0:T(8,128)(2,1)S(1)}, bf16[8,64,128]{2,1,0:T(8,128)(2,1)S(1)}) custom-call(bf16[8,4096,128]{2,1,0:T(8,128)(2,1)} %basis.1, bf16[8,4096,128]{2,1,0:T(8,128)(2,1)} %image.1, s32[8,64]{1,0:T(8,128)} %selection.1), custom_call_target="tpu_custom_call" | custom-call | tf_op jit(solution)/shard_map/pallas_call | solution.py:459
  32.7 5.6 %shard_map.38 = bf16[8,4096,128]{2,1,0:T(8,128)(2,1)} custom-call(bf16[8,4096,128]{2,1,0:T(8,128)(2,1)S(1)} %get-tuple-element.8.basis, bf16[8,4096,128]{2,1,0:T(8,128)(2,1)S(1)} %get-tuple-element.9.image, bf16[8,64,128]{2,1,0:T(8,128)(2,1)S(1)} %get-tuple-element.10.coeffs), custom_call_target="tpu_custom_call" | custom-call | tf_op jit(solution)/shard_map/pallas_call | solution.py:486

commit v3 on v2

--- a/solution.py
+++ b/solution.py
@@ -158,7 +158,7 @@
 
 
 def coeff_kernel(
-    sizes, total_rows, basis, image, selection, held_w, held_q, out, shared, chosen,
+    sizes, total_rows, basis, image, selection, held_w, held_q, out, shared, chosen, raw,
     f_own, f_core, f_plane, f_deep, x_top, x_top_core, x_top_plane, x_top_deep,
     x_low, x_low_core, x_low_plane, x_low_deep, s_own, s_core, s_plane, s_deep,
     load_w, load_q, core_send, core_recv, plane_send, plane_recv, deep_send, deep_recv, csend, crecv, load_c
@@ -318,24 +318,31 @@
                 if g * batch + u < nsys - 1:
                     in_plane(0, g * batch + u - half).start()
 
+    def pack_s(spots):
+        for u, s in enumerate(spots):
+            mixed, diag = symmetric_pack(raw[u])
+            s_own[s, 0 : width // 2, :] = mixed
+            s_own[s, width // 2 :, :] = diag
+
     def second_gram(g):
         spots = [at(g * batch + u) for u in range(batch)]
         for s in spots:
             load(basis, held_w, load_w, s).wait()
         issue(g + groups)
-        for s in spots:
+        for u, s in enumerate(spots):
             left = held_w[s]
             pair = gram_of(left, jnp.concatenate([left, held_q[s]], axis=1))
-            mixed, diag = symmetric_pack(pair[:, :width])
-            s_own[s, 0 : width // 2, :] = mixed
-            s_own[s, width // 2 :, :] = diag
+            raw[u] = pair[:, :width]
             x_top[s] = pair[: width // 2, width:]
             x_low[s, 0 : width // 2, :] = pair[width // 2 :, width:]
             x_low[s, width // 2 :, :] = diagonal_row(pair[:, :width])
         if g < groups // 2:
             for s in spots:
-                for kind in (1, 2, 3):
+                for kind in (1, 2):
                     to_core(kind, s).start()
+            pack_s(spots)
+            for s in spots:
+                to_core(3, s).start()
         else:
             for kind in (1, 2):
                 for u, s in enumerate(spots):
@@ -344,6 +351,7 @@
                     own[s] += got[lax.rem(s, half)]
                     if g * batch + u < nsys - 1:
                         in_plane(kind, g * batch + u - half).start()
+            pack_s(spots)
             for u, s in enumerate(spots):
                 to_core(3, s).wait_recv()
                 s_own[s] += s_core[lax.rem(s, half)]
@@ -464,6 +472,7 @@
         scratch_shapes=[
             pltpu.VMEM((nsys, keep, width), jnp.bfloat16),
             pltpu.VMEM((nsys, keep), jnp.int32),
+            pltpu.VMEM((max(BATCH, 1), width, width), jnp.float32),
             *buffers,
             pltpu.SemaphoreType.DMA((nsys,)),
             pltpu.SemaphoreType.DMA((nsys,)),

time: 38.7 us -> 38.6 us (level)
  no operation moved by 1% of the time
where the time goes in v3:
time: 38.6 us; the launch traced here: 38.5 us
  Pallas kernels  38.3 us (99%)
    pallas_call x1, Pallas kernels, on_device(): pl.pallas_call(functools.partial(coeff_kernel, (n_rows, n_groups), total_...  32.6 us
    pallas_call x1, Pallas kernels, on_device(): pl.pallas_call(rotate_kernel, in_specs=[in_vmem, in_vmem, in_vmem], out_s...  5.62 us

profile of v3, /device:TPU:0, one launch (start us, length us, event | category | flops | bytes accessed | tf_op | source)
XLA Modules:
  0.0 38.5 jit_solution(16133791202525257832)
XLA Ops:
  0.0 32.6 %shard_map.37 = (bf16[8,4096,128]{2,1,0:T(8,128)(2,1)S(1)}, bf16[8,4096,128]{2,1,0:T(8,128)(2,1)S(1)}, bf16[8,64,128]{2,1,0:T(8,128)(2,1)S(1)}) custom-call(bf16[8,4096,128]{2,1,0:T(8,128)(2,1)} %basis.1, bf16[8,4096,128]{2,1,0:T(8,128)(2,1)} %image.1, s32[8,64]{1,0:T(8,128)} %selection.1), custom_call_target="tpu_custom_call" | custom-call | tf_op jit(solution)/shard_map/pallas_call | solution.py:467
  32.6 5.6 %shard_map.38 = bf16[8,4096,128]{2,1,0:T(8,128)(2,1)} custom-call(bf16[8,4096,128]{2,1,0:T(8,128)(2,1)S(1)} %get-tuple-element.8.basis, bf16[8,4096,128]{2,1,0:T(8,128)(2,1)S(1)} %get-tuple-element.9.image, bf16[8,64,128]{2,1,0:T(8,128)(2,1)S(1)} %get-tuple-element.10.coeffs), custom_call_target="tpu_custom_call" | custom-call | tf_op jit(solution)/shard_map/pallas_call | solution.py:495
